TPU v7x, 32 devices: a whole 2x2x4 slice. The times are simulated.
32 devices in a mesh: row: 8 (over z, core), col: 4 (over y, x).
Axes of the slice: x: 2, y: 2, z: 4, core: 2. Of those that a mesh axis runs over, the one named last changes fastest.
Arguments:
- pair_exchange: bfloat16 [64, 16, 1024], P(('row', 'col')), may hold values from -6 to 6
- conduction: bfloat16 [64, 4, 1024], P(('row', 'col')), may hold values from -6 to 6
- valence: bfloat16 [64, 4, 1024], P(('row', 'col')), may hold values from -6 to 6
- coulomb: float32 [1024], replicated, may hold values from 0.5 to 5
- screening: float32 [34, 1024], replicated, may hold values from 0.1 to 1
- energies: float32 [64, 16], P(('row', 'col')), may hold values from 1 to 9
- vectors: bfloat16 [64, 512], P(('row', 'col')), may hold values from -6 to 6
- k_coords: int32 [64, 2], P(('row', 'col')), may hold values from 0 to 31, as said below
Outputs:
- residual_block: float32 [64, 512], P(('row', 'col'))
- alpha: float32 [32, 32], replicated
Inputs may be any that keep to these rules, and one draw needn't show every extreme that they name: `k_coords`: each row holds a k-point's coordinates on the periodic 32 x 2 mesh, first then second; every mesh point occurs exactly once.
All inputs are finite; a program needn't handle non-finite values.
Results may differ from a plain program's by a relative error of at most 0.0028.
Values may be sent and summed in bfloat16 or wider, within the bound.
A program may use at most 64 MiB of HBM per device.

v0:
```python
import jax
import jax.numpy as jnp
from jax import lax
from jax.sharding import PartitionSpec as P

MX = 32


highest = lax.Precision.HIGHEST


def pair_factors(conduction, valence):
    count, valence_count, plane_count = valence.shape
    joined = (
        valence.astype(jnp.float32)[:, :, None, :] * conduction.astype(jnp.float32)[:, None, :, :]
    )
    return joined.reshape(count, valence_count * conduction.shape[1], plane_count).astype(
        jnp.bfloat16
    )


def transfer_index(rows_at, cols_at, mesh_cols):
    delta_first = jnp.mod(rows_at[:, None, 0] - cols_at[None, :, 0], MX)
    delta_second = jnp.mod(rows_at[:, None, 1] - cols_at[None, :, 1], mesh_cols)
    fold_first = jnp.minimum(delta_first, MX - delta_first)
    fold_second = jnp.minimum(delta_second, mesh_cols - delta_second)
    return (fold_first * (mesh_cols // 2 + 1) + fold_second).astype(jnp.int32)


def on_device(pair_exchange, conduction, valence, coulomb, screening, energies, vectors, k_coords):
    local_count, band_count, plane_count = pair_exchange.shape
    vector_count = vectors.shape[1] // band_count
    row_count = lax.axis_size("row")
    col_count = lax.axis_size("col")
    total_count = local_count * row_count * col_count
    mesh_cols = total_count // MX
    moving = vectors.reshape(local_count, band_count, vector_count)
    partial_density = jnp.einsum(
        "ktg,ktn->gn", pair_exchange, moving, preferred_element_type=jnp.float32
    )
    density = lax.psum(partial_density, ("row", "col"))
    block_size = 128
    sweeps = plane_count // block_size
    col_cond, col_val, col_vec, col_at = (
        lax.all_gather(conduction, "row", axis=0, tiled=True),
        lax.all_gather(valence, "row", axis=0, tiled=True),
        lax.all_gather(vectors, "row", axis=0, tiled=True),
        lax.all_gather(k_coords, "row", axis=0, tiled=True),
    )
    row_cond, row_val, row_at = (
        lax.all_gather(conduction, "col", axis=0, tiled=True),
        lax.all_gather(valence, "col", axis=0, tiled=True),
        lax.all_gather(k_coords, "col", axis=0, tiled=True),
    )
    row_pairs = pair_factors(row_cond, row_val)
    col_pairs = pair_factors(col_cond, col_val)
    indices = transfer_index(row_at, col_at, mesh_cols)
    col_moving = col_vec.reshape(-1, band_count, vector_count)

    def square_sweep(sweep_index, running):
        anchor = sweep_index * block_size
        coupling = jnp.take(
            lax.dynamic_slice_in_dim(screening, anchor, block_size, 1), indices, axis=0
        )
        row_block = lax.dynamic_slice_in_dim(row_pairs, anchor, block_size, 2)
        col_block = lax.dynamic_slice_in_dim(col_pairs, anchor, block_size, 2)
        col_proj = jnp.einsum(
            "ktg,ktn->kng", col_block, col_moving, preferred_element_type=jnp.float32
        )
        potential = jnp.einsum("ijg,jng->ing", coupling, col_proj, precision=highest)
        return running + jnp.einsum(
            "ktg,kng->ktn", row_block.astype(jnp.float32), potential, precision=highest
        )

    forward = lax.fori_loop(
        0,
        sweeps,
        square_sweep,
        jnp.zeros((row_pairs.shape[0], band_count, vector_count), jnp.float32),
    )
    owned = lax.psum_scatter(
        forward.reshape(col_count, local_count, band_count, vector_count),
        "col",
        scatter_dimension=0,
        tiled=True,
    )[0]
    moving_wide = moving.astype(jnp.float32)
    exchange_term = jnp.einsum(
        "ktg,gn->ktn", pair_exchange.astype(jnp.float32) * coulomb, density, precision=highest
    )
    applied = (
        energies[:, :, None] * moving_wide
        + 2.0 / (total_count * band_count) * exchange_term
        - owned / total_count
    )
    gram = jnp.einsum("ktm,ktn->mn", moving_wide, applied, precision=highest)
    alpha = lax.psum(gram, ("row", "col")) / (total_count * band_count)
    residual = applied - jnp.einsum("ktm,mn->ktn", moving_wide, alpha, precision=highest)
    return (residual.reshape(local_count, band_count * vector_count), alpha)


def solution(mesh):
    in_specs = (
        P(("row", "col"), None, None),
        P(("row", "col"), None, None),
        P(("row", "col"), None, None),
        P(),
        P(),
        P(("row", "col"), None),
        P(("row", "col"), None),
        P(("row", "col"), None),
    )
    out_specs = (P(("row", "col"), None), P())
    return jax.shard_map(
        on_device, mesh=mesh, in_specs=in_specs, out_specs=out_specs, check_vma=False
    )
```

profile of v0, /device:TPU:0, one launch (start us, length us, event | category | flops | bytes accessed | tf_op | source)
XLA Modules:
  0.0 299.9 jit_solution(13418184121838847277)
XLA Ops:
  8.7 13.5 %all-gather.2 = s32[8,2,2]{2,1,0:T(2,128)S(1)} all-gather(s32[1,2,2]{2,1,0:T(2,128)S(1)} %bitcast.65), channel_id=1, replica_groups=mesh['row'=8,'col'=4] {'row'}, dimensions={0}, use_global_device_ids=true | all-gather | bytes 144 | tf_op jit(solution)/shard_map/all_gather | solution.py:48
  22.1 8.1 %all-gather.1 = s32[4,2,2]{2,1,0:T(2,128)S(1)} all-gather(s32[1,2,2]{2,1,0:T(2,128)S(1)} %bitcast.66), channel_id=1, replica_groups=mesh['row'=8,'col'=4] {'col'}, dimensions={0}, use_global_device_ids=true | all-gather | bytes 80 | tf_op jit(solution)/shard_map/all_gather | solution.py:53
  30.2 14.3 %all_gather.23 = bf16[16,4,1024]{2,1,0:T(4,128)(2,1)S(1)} all-gather(bf16[2,4,1024]{2,1,0:T(4,128)(2,1)} %param.12), channel_id=1, replica_groups=mesh['row'=8,'col'=4] {'row'}, dimensions={0}, use_global_device_ids=true | all-gather | bytes 147456 | tf_op jit(solution)/shard_map/all_gather | solution.py:46
  44.5 8.3 %all_gather.21 = bf16[8,4,1024]{2,1,0:T(4,128)(2,1)S(1)} all-gather(bf16[2,4,1024]{2,1,0:T(4,128)(2,1)S(1)} %copy-done.2), channel_id=1, replica_groups=mesh['row'=8,'col'=4] {'col'}, dimensions={0}, use_global_device_ids=true | all-gather | bytes 81920 | tf_op jit(solution)/shard_map/all_gather | solution.py:52
  52.9 14.0 %all_gather.24 = bf16[16,4,1024]{2,1,0:T(4,128)(2,1)S(1)} all-gather(bf16[2,4,1024]{2,1,0:T(4,128)(2,1)S(1)} %copy-done.3), channel_id=1, replica_groups=mesh['row'=8,'col'=4] {'row'}, dimensions={0}, use_global_device_ids=true | all-gather | bytes 147456 | tf_op jit(solution)/shard_map/all_gather | solution.py:45
  66.9 7.2 %all_gather.22 = bf16[8,4,1024]{2,1,0:T(4,128)(2,1)S(1)} all-gather(bf16[2,4,1024]{2,1,0:T(4,128)(2,1)S(1)} %copy-done.3), channel_id=1, replica_groups=mesh['row'=8,'col'=4] {'col'}, dimensions={0}, use_global_device_ids=true | all-gather | bytes 81920 | tf_op jit(solution)/shard_map/all_gather | solution.py:51
  75.8 12.8 %all-gather = bf16[8,2,512]{2,1,0:T(2,128)(2,1)S(1)} all-gather(bf16[1,2,512]{2,1,0:T(2,128)(2,1)S(1)} %bitcast.64), channel_id=1, replica_groups=mesh['row'=8,'col'=4] {'row'}, dimensions={0}, use_global_device_ids=true | all-gather | bytes 18432 | tf_op jit(solution)/shard_map/all_gather | solution.py:47
  88.7 33.2 %while.14 = (s32[]{:T(128)}, f32[8,16,32]{2,1,0:T(8,128)S(1)}, bf16[8,16,1024]{2,1,0:T(8,128)(2,1)S(1)}, bf16[16,16,1024]{2,1,0:T(8,128)(2,1)S(1)}, bf16[16,16,3...) while((s32[]{:T(128)}, f32[8,16,32]{2,1,0:T(8,128)S(1)}, ...), condition=%wide.region_2.3_spmd.clone, body=%wide.region_1.2_spmd.clone.sunk | while | flops 14714503 | bytes 2319689 | solution.py:75
  88.7 0.7 constant_dynamic-slice_fusion.2
  91.4 1.1 convolution_bitcast_fusion.8
  92.9 0.7 constant_dynamic-slice_fusion.2
  95.5 1.1 convolution_bitcast_fusion.8
  97.0 0.7 constant_dynamic-slice_fusion.2
  97.9 0.6 gather_fusion
  99.7 1.1 convolution_bitcast_fusion.8
  101.2 0.7 constant_dynamic-slice_fusion.2
  103.8 1.1 convolution_bitcast_fusion.8
  105.3 0.7 constant_dynamic-slice_fusion.2
  108.0 1.1 convolution_bitcast_fusion.8
  109.5 0.7 constant_dynamic-slice_fusion.2
  112.1 1.1 convolution_bitcast_fusion.8
  113.6 0.7 constant_dynamic-slice_fusion.2
  116.3 1.1 convolution_bitcast_fusion.8
  117.8 0.7 constant_dynamic-slice_fusion.2
  120.4 1.1 convolution_bitcast_fusion.8
  122.8 0.9 convolution_bitcast_fusion.2
  123.7 20.7 %reduce-scatter.4.cloned.1.call-done = f32[1,2,16,32]{3,2,1,0:T(8,128)} async-done(((f32[4,2,16,32]{3,2,1,0:T(8,128)}), f32[1,2,16,32]{3,2,1,0:T(8,128)}) %reduce-scatter.4.cloned.1.call-update) | async-done | bytes 4112
  144.4 105.9 %all-reduce.3.cloned.1.call-done = f32[1024,32]{0,1:T(8,128)} async-done(((f32[1024,32]{0,1:T(8,128)}), f32[1024,32]{0,1:T(8,128)}) %all-reduce.3.cloned.1.call-update) | async-done | bytes 131088 | tf_op jit(solution)/shard_map/psum | solution.py:41
  250.3 1.1 fusion.17
  251.7 39.3 %psum.15 = f32[32,32]{0,1:T(8,128)S(1)} all-reduce(f32[32,32]{0,1:T(8,128)S(1)} %convolution_bitcast_fusion.4), channel_id=1, replica_groups=mesh['row'=8,'col'=4] {'row','col'}, use_global_device_ids=true, to_apply=%region_4.5 | all-reduce | flops 1024 | bytes 8192 | tf_op jit(solution)/shard_map/psum | solution.py:97
  291.1 0.7 reshape.61
  291.8 0.7 copy.24
  (111 shorter events, 21.2 us)
Async XLA Ops:
  8.0 0.7 copy-start.6
  8.0 136.4 %reduce-scatter.4.cloned.1.call-start = ((), (), s32[]{:S(2)}) async-start(), calls=%async_computation.2 | async-start | bytes 81920
  30.2 14.3 %copy-start.2 = (bf16[2,4,1024]{2,1,0:T(4,128)(2,1)S(1)}, bf16[2,4,1024]{2,1,0:T(4,128)(2,1)}, u32[]{:S(2)}) copy-start(bf16[2,4,1024]{2,1,0:T(4,128)(2,1)} %param.12) | copy-start | bytes 49156
  44.5 8.3 %copy-start.3 = (bf16[2,4,1024]{2,1,0:T(4,128)(2,1)S(1)}, bf16[2,4,1024]{2,1,0:T(4,128)(2,1)}, u32[]{:S(2)}) copy-start(bf16[2,4,1024]{2,1,0:T(4,128)(2,1)} %param.11) | copy-start | bytes 49156
  75.2 0.7 copy-start.4
  121.9 0.6 copy-start
  121.9 0.9 copy-start.1
  122.6 127.7 %all-reduce.3.cloned.1.call-start = ((), (), s32[]{:S(2)}) async-start(), calls=%async_computation.1 | async-start | bytes 262144 | tf_op jit(solution)/shard_map/psum | solution.py:41
  123.7 126.6 %copy-start.5 = (f32[1024]{0:T(1024)S(1)}, f32[1024]{0:T(1024)}, u32[]{:S(2)}) copy-start(f32[1024]{0:T(1024)} %param.13) | copy-start | bytes 12292
  123.7 126.6 %copy-start.7 = (f32[2,16]{1,0:T(2,128)S(1)}, f32[2,16]{1,0:T(2,128)}, u32[]{:S(2)}) copy-start(f32[2,16]{1,0:T(2,128)} %param.15) | copy-start | bytes 388
Sparse Core Ops, SparseCore 0:
  122.7 21.6 reduce-scatter.3
Sparse Core Ops, SparseCore 1:
  128.6 121.6 all-reduce.2
where the time goes:
time: 301 us; the launch traced here: 300 us
  waiting for transfers between devices  127 us (42%)
  blocking collectives  117 us (39%)
  local copies, waits for them, and re-layouts  21.7 us (7%)
  matrix products  16.1 us (5%)
  between operations  15.6 us (5%)
    psum x1, waiting for transfers between devices, on_device(): density = lax.psum(partial_density, ('row', 'col'))  106 us
    psum x1, blocking collectives, on_device(): alpha = lax.psum(gram, ('row', 'col')) / (total_count * band_count)  39.3 us
    unnamed x3, waiting for transfers between devices  20.8 us
    all_gather x1, blocking collectives, on_device(): lax.all_gather(valence, 'row', axis=0, tiled=True)  14.3 us
    all_gather x1, blocking collectives, on_device(): lax.all_gather(conduction, 'row', axis=0, tiled=True)  14 us
    all_gather x1, blocking collectives, on_device(): lax.all_gather(k_coords, 'row', axis=0, tiled=True)  13.5 us
    all_gather x1, blocking collectives, on_device(): lax.all_gather(vectors, 'row', axis=0, tiled=True)  12.8 us
    dot_general x8, matrix products, square_sweep(): jnp.einsum('ijg,jng->ing', coupling, col_proj, precision=highest)  8.7 us
  transfers between devices with their start and end apart: 2, of which 2 were waited for; matrix products, arithmetic and copies ran while one was open for 0% of the time, Pallas kernels for 0%

commit v1 on v0

--- a/solution.py
+++ b/solution.py
@@ -1,9 +1,339 @@
+import functools
+
 import jax
 import jax.numpy as jnp
 from jax import lax
+from jax.experimental import pallas as pl
+from jax.experimental.pallas import tpu as pltpu
 from jax.sharding import PartitionSpec as P
 
 MX = 32
+LANES = 128
+MESH = pl.DeviceIdType.MESH
+F32 = jnp.float32
+BF16 = jnp.bfloat16
+
+
+def split_pair(value):
+    high = value.astype(BF16)
+    return high, (value - high.astype(F32)).astype(BF16)
+
+
+def dot(a, b, contract):
+    return lax.dot_general(a, b, ((contract[0:1], contract[1:2]), ((), ())), preferred_element_type=F32)
+
+
+def iota(shape, axis):
+    return lax.broadcasted_iota(jnp.int32, shape, axis)
+
+
+def one_hot(condition):
+    return jnp.where(condition, 1.0, 0.0).astype(BF16)
+
+
+def kernel(
+    dims, msg_ref, px_ref, wide_ref, coulomb_ref, screening_ref,
+    out_ref, alpha_ref,
+    slots, px_slots, sel_v, sel_c, tile_m, block_m, perm, sel_k, screen, tiled, pairs, proj, coords, coupling,
+    dens_slots, partial, out_send, out_slots, gram_slots,
+    in_send, in_recv, px_send, px_recv, dens_send, dens_recv, gram_send, gram_recv, o_send, o_recv,
+):
+    rows, cols, nk, nv, nc, nvec, total, mesh_cols = dims
+    row, col = lax.axis_index("row"), lax.axis_index("col")
+    me = row * cols + col
+    count = rows * cols
+    kb = rows * nk
+    nb = nv * nc
+    unit = nk * nv
+    per = kb * nv
+    batch = per * nc
+
+    def other(step):
+        peer = lax.rem(me + step, count)
+        return peer // cols, lax.rem(peer, cols)
+
+    barrier = pltpu.get_barrier_semaphore()
+
+    def greet(step, carry):
+        pr, pc = other(step)
+        pl.semaphore_signal(barrier, inc=1, device_id=(pr, pc), device_id_type=MESH)
+        return carry
+
+    lax.fori_loop(1, count, greet, 0)
+
+    at = iota((batch, rows * 16), 0)
+    to = iota((batch, rows * 16), 1)
+    base = (at // unit) % rows * 16 + (at // nv) % nk * 8
+    sel_v[...] = one_hot(to == base + at % nv)
+    sel_c[...] = one_hot(to == base + nv + at // per)
+    at = iota((LANES, nc * LANES), 0)
+    to = iota((LANES, nc * LANES), 1)
+    tile_m[...] = one_hot((at // nvec == to // LANES) & (at % nvec == to % nvec))
+    at = iota((batch, kb * nvec), 0)
+    to = iota((batch, kb * nvec), 1)
+    block_m[...] = one_hot((at // nv) % kb == to // nvec)
+    at = iota((batch, rows * nk * nb), 0)
+    to = iota((batch, rows * nk * nb), 1)
+    perm[...] = one_hot(to == (at // nv) % kb * nb + at % nv * nc + at // per)
+    at = iota((2 * cols * kb, count * 8), 0)
+    to = iota((2 * cols * kb, count * 8), 1)
+    point = at % (cols * kb)
+    sel_k[...] = one_hot(to == point // nk * 8 + at // (cols * kb) * nk + point % nk)
+    screen[...] = jnp.zeros_like(screen)
+    mine = pl.ds(pl.multiple_of(row * LANES, LANES), LANES)
+    high, low = split_pair(jnp.concatenate(
+        [screening_ref[:, mine], jnp.zeros((LANES - screening_ref.shape[0], LANES), F32)], axis=0))
+    screen[0:LANES] = high
+    screen[LANES:2 * LANES] = low
+
+    pl.semaphore_wait(barrier, count - 1)
+
+    def in_copy(step):
+        pr, pc = other(step)
+        return pltpu.make_async_remote_copy(
+            src_ref=msg_ref.at[pr], dst_ref=slots.at[col, row],
+            send_sem=in_send.at[pc, pr], recv_sem=in_recv.at[col, row],
+            device_id=(pr, pc), device_id_type=MESH)
+
+    def px_copy(step):
+        pr = lax.rem(row + step, rows)
+        return pltpu.make_async_remote_copy(
+            src_ref=px_ref.at[:, :, pl.ds(pl.multiple_of(pr * LANES, LANES), LANES)], dst_ref=px_slots.at[row],
+            send_sem=px_send.at[pr], recv_sem=px_recv.at[row],
+            device_id=(pr, col), device_id_type=MESH)
+
+    def dens_copy(step):
+        pc = lax.rem(col + step, cols)
+        return pltpu.make_async_remote_copy(
+            src_ref=dens_slots.at[col], dst_ref=dens_slots.at[col],
+            send_sem=dens_send.at[pc], recv_sem=dens_recv.at[col],
+            device_id=(row, pc), device_id_type=MESH)
+
+    def gram_copy(step):
+        pr, pc = other(step)
+        return pltpu.make_async_remote_copy(
+            src_ref=gram_slots.at[me], dst_ref=gram_slots.at[me],
+            send_sem=gram_send.at[pr * cols + pc], recv_sem=gram_recv.at[me],
+            device_id=(pr, pc), device_id_type=MESH)
+
+    def o_copy(step):
+        pr = lax.rem(row + step, rows)
+        return pltpu.make_async_remote_copy(
+            src_ref=out_send.at[pr], dst_ref=out_slots.at[row],
+            send_sem=o_send.at[pr], recv_sem=o_recv.at[row],
+            device_id=(pr, col), device_id_type=MESH)
+
+    def start_all(copy, end):
+        def body(step, carry):
+            copy(step).start()
+            return carry
+        lax.fori_loop(1, end, body, 0)
+
+    def landed(ref, sem):
+        pltpu.make_async_copy(ref, ref, sem).wait()
+
+    start_all(px_copy, rows)
+    start_all(in_copy, count)
+    slots[col, row] = msg_ref[row]
+    px_slots[row] = px_ref[:, :, mine]
+
+    def take_batch(which):
+        def wait_one(r, carry):
+            @pl.when((r != row) | (which != col))
+            def _():
+                landed(slots.at[which, r], in_recv.at[which, r])
+            return carry
+        lax.fori_loop(0, rows, wait_one, 0)
+        got = slots[which]
+        factors = got[:, 0:16, :].reshape(rows * 16, LANES)
+        rest = got[:, 16:32, :].astype(F32)
+        packed = rest[:, 0:8, :].reshape(per, LANES).astype(BF16)
+        coords[which] = rest[:, 8:16, :].reshape(rows * 8, LANES).astype(BF16)
+        wide = dot(packed, tile_m[...], (1, 0)).astype(BF16)
+        stacked = jnp.concatenate([wide[:, s * LANES:(s + 1) * LANES] for s in range(nc)], axis=0)
+        tiled[which] = stacked
+        joined = (dot(sel_v[...], factors, (1, 0)) * dot(sel_c[...], factors, (1, 0))).astype(BF16)
+        pairs[which] = joined.astype(F32)
+        spread = jnp.concatenate([stacked] * (kb * nvec // LANES), axis=1) * block_m[...]
+        projected = dot(spread, joined, (0, 0))
+        proj[pl.ds(which * kb, kb)] = projected.reshape(kb, nvec, LANES)
+
+    take_batch(col)
+
+    def px_wait(step, carry):
+        r = lax.rem(row + step, rows)
+        landed(px_slots.at[r], px_recv.at[r])
+        return carry
+
+    lax.fori_loop(1, rows, px_wait, 0)
+    px = dot(perm[...], px_slots[...].reshape(rows * nk * nb, LANES), (1, 0)).astype(BF16)
+    own_x = tiled[col][:, 0:nvec]
+    dens_slots[col] = dot(own_x, px, (0, 0))
+    start_all(dens_copy, cols)
+
+    def rest_batches(step, carry):
+        take_batch(lax.rem(col + step, cols))
+        return carry
+
+    lax.fori_loop(1, cols, rest_batches, 0)
+
+    place = dot(sel_k[...], coords[...].reshape(count * 8, LANES), (1, 0))
+    points = cols * kb
+    first, second = place[0:points], place[points:2 * points]
+    lane = iota((points, LANES), 1).astype(F32)
+    coupling[0, 0:points] = first
+    coupling[1, 0:points] = second
+    start = pl.multiple_of(col * kb, kb)
+    own_first = coupling[0, pl.ds(start, kb), :]
+    own_second = coupling[1, pl.ds(start, kb), :]
+    hots = []
+    for i in range(kb):
+        da = jnp.abs(own_first[i:i + 1] - first)
+        db = jnp.abs(own_second[i:i + 1] - second)
+        q = jnp.minimum(da, MX - da) * (mesh_cols // 2 + 1) + jnp.minimum(db, mesh_cols - db)
+        hots.append(one_hot(q == lane))
+    for i in range(kb):
+        coupling[i] = dot(jnp.concatenate([hots[i], hots[i]], axis=1), screen[...], (1, 0))
+
+    def dens_wait(step, carry):
+        c = lax.rem(col + step, cols)
+        landed(dens_slots.at[c], dens_recv.at[c])
+        return carry
+
+    lax.fori_loop(1, cols, dens_wait, 0)
+    density = dens_slots[0]
+    for c in range(1, cols):
+        density = density + dens_slots[c]
+    high, low = split_pair(density * coulomb_ref[:, mine] * (2.0 / (total * nb)))
+    partial[...] = (dot(px, high, (1, 1)) + dot(px, low, (1, 1))).reshape(nc, rows, unit, nvec)
+
+    wide_own = wide_ref[...] * msg_ref[row, 16:32, :].astype(F32)[0:8]
+    for s in range(nc):
+        partial[s, row] = partial[s, row] + wide_own[:, s * nvec:(s + 1) * nvec]
+
+    group = 4
+    row_k = (iota((nc * unit, LANES), 0) // nv) % nk
+    potentials = []
+    for block in range(kb // group):
+        def gather(j, sums):
+            term = proj[j]
+            return tuple(
+                sums[u] + coupling[block * group + u, pl.ds(j, 1), :] * term for u in range(group))
+        potentials += list(lax.fori_loop(
+            0, points, gather, tuple(jnp.zeros((nvec, LANES), F32) for _ in range(group)), unroll=8))
+    for r in range(rows):
+        mine_pairs = pairs[col].reshape(nc, rows, unit, LANES)[:, r].reshape(nc * unit, LANES)
+        left = jnp.concatenate(
+            [jnp.where(row_k == k, mine_pairs, 0.0) for k in range(nk)], axis=1).astype(BF16)
+        high, low = split_pair(jnp.concatenate([potentials[r * nk + k] for k in range(nk)], axis=1))
+        direct = dot(left, high, (1, 1)) + dot(left, low, (1, 1))
+        for s in range(nc):
+            partial[s, r] = partial[s, r] - direct[s * unit:(s + 1) * unit] * (1.0 / total)
+
+    whole = partial[...]
+    packed = jnp.concatenate([whole[s].reshape(per, nvec) for s in range(nc)], axis=1)
+    out_send[...] = packed.reshape(rows, unit, LANES)
+    start_all(o_copy, rows)
+    high, low = split_pair(whole.reshape(batch, nvec))
+    gram = dot(own_x, high, (0, 0)) + dot(own_x, low, (0, 0))
+    step = nvec // nc
+    gram_slots[me] = jnp.concatenate([gram[s * step:(s + 1) * step] for s in range(nc)], axis=1)
+    start_all(gram_copy, count)
+
+    def o_wait(d, acc):
+        r = lax.rem(row + d, rows)
+        landed(out_slots.at[r], o_recv.at[r])
+        return acc + out_slots[r]
+
+    applied = lax.fori_loop(1, rows, o_wait, out_send[row])
+
+    def gram_wait(d, carry):
+        p = lax.rem(me + d, count)
+        landed(gram_slots.at[p], gram_recv.at[p])
+        return carry
+
+    lax.fori_loop(1, count, gram_wait, 0)
+    sums = jnp.sum(gram_slots[...], axis=0) * (1.0 / (total * nb))
+    alpha = jnp.concatenate([sums[:, s * nvec:(s + 1) * nvec] for s in range(nc)], axis=0)
+    alpha_ref[...] = alpha
+    own = msg_ref[row, 16:32, :].astype(F32)[0:8]
+    own_rows = jnp.concatenate([own[:, s * nvec:(s + 1) * nvec] for s in range(nc)], axis=0).astype(BF16)
+    high, low = split_pair(alpha)
+    taken = dot(own_rows, high, (1, 0)) + dot(own_rows, low, (1, 0))
+    residual = applied - jnp.concatenate([taken[s * unit:(s + 1) * unit] for s in range(nc)], axis=1)
+    for j in range(nv):
+        out_ref[:, j * LANES:(j + 1) * LANES] = jnp.concatenate(
+            [residual[k * nv + j:k * nv + j + 1] for k in range(nk)], axis=0)
+
+    def drain(copy, end):
+        def body(d, carry):
+            copy(d).wait_send()
+            return carry
+        lax.fori_loop(1, end, body, 0)
+
+    drain(in_copy, count)
+    drain(px_copy, rows)
+    drain(dens_copy, cols)
+    drain(o_copy, rows)
+    drain(gram_copy, count)
+
+
+def fast_on_device(pair_exchange, conduction, valence, coulomb, screening, energies, vectors, k_coords):
+    nk, nb, planes = pair_exchange.shape
+    nv, nc = valence.shape[1], conduction.shape[1]
+    nvec = vectors.shape[1] // nb
+    rows, cols = lax.axis_size("row"), lax.axis_size("col")
+    count = rows * cols
+    total = nk * count
+    unit = nk * nv
+    kb = rows * nk
+    batch = kb * nb
+    factors = jnp.concatenate([valence, conduction], axis=1).reshape(nk * (nv + nc), rows, LANES)
+    packed = vectors.reshape(unit, LANES)
+    spots = jnp.broadcast_to(k_coords.T.astype(BF16).reshape(2 * nk, 1), (2 * nk, LANES))
+    extra = jnp.concatenate([packed, spots, jnp.zeros((16 - unit - 2 * nk, LANES), BF16)], axis=0)
+    message = jnp.concatenate(
+        [factors.transpose(1, 0, 2), jnp.broadcast_to(extra[None], (rows, 16, LANES))], axis=1)
+    wide = jnp.repeat(energies.reshape(unit, nc), nvec, axis=1)
+    vmem = pl.BlockSpec(memory_space=pltpu.VMEM)
+    dma = pltpu.SemaphoreType.DMA
+    points = cols * kb
+    return pl.pallas_call(
+        functools.partial(kernel, (rows, cols, nk, nv, nc, nvec, total, total // MX)),
+        out_shape=(
+            jax.ShapeDtypeStruct((nk, nb * nvec), F32),
+            jax.ShapeDtypeStruct((nvec, nvec), F32),
+        ),
+        in_specs=[vmem] * 5,
+        out_specs=(vmem, vmem),
+        scratch_shapes=[
+            pltpu.VMEM((cols, rows, 32, LANES), BF16),
+            pltpu.VMEM((rows, nk, nb, LANES), BF16),
+            pltpu.VMEM((batch, rows * 16), BF16),
+            pltpu.VMEM((batch, rows * 16), BF16),
+            pltpu.VMEM((LANES, nc * LANES), BF16),
+            pltpu.VMEM((batch, kb * nvec), BF16),
+            pltpu.VMEM((batch, batch), BF16),
+            pltpu.VMEM((2 * points, count * 8), BF16),
+            pltpu.VMEM((2 * LANES, LANES), BF16),
+            pltpu.VMEM((cols, batch, LANES), BF16),
+            pltpu.VMEM((cols, batch, LANES), F32),
+            pltpu.VMEM((points, nvec, LANES), F32),
+            pltpu.VMEM((cols, rows * 8, LANES), BF16),
+            pltpu.VMEM((kb, points, LANES), F32),
+            pltpu.VMEM((cols, nvec, LANES), F32),
+            pltpu.VMEM((nc, rows, unit, nvec), F32),
+            pltpu.VMEM((rows, unit, LANES), F32),
+            pltpu.VMEM((rows, unit, LANES), F32),
+            pltpu.VMEM((count, nvec // nc, LANES), F32),
+            dma((cols, rows)), dma((cols, rows)),
+            dma((rows,)), dma((rows,)),
+            dma((cols,)), dma((cols,)),
+            dma((count,)), dma((count,)),
+            dma((rows,)), dma((rows,)),
+        ],
+        compiler_params=pltpu.CompilerParams(collective_id=0, has_side_effects=True),
+    )(message, pair_exchange, wide, coulomb.reshape(1, planes), screening)
 
 
 highest = lax.Precision.HIGHEST
@@ -99,6 +429,20 @@
     return (residual.reshape(local_count, band_count * vector_count), alpha)
 
 
+def fits(args, mesh):
+    pair_exchange, conduction, valence, _, screening, _, vectors, _ = args
+    rows, cols = mesh.shape["row"], mesh.shape["col"]
+    points, nb, planes = pair_exchange.shape
+    nk = points // (rows * cols)
+    nv, nc = valence.shape[1], conduction.shape[1]
+    nvec = vectors.shape[1] // nb
+    return (
+        planes == rows * LANES and nc * nvec == LANES and nk * nv == 8 and nk * (nv + nc) == 16
+        and nk == 2 and nvec // nc == 8 and rows % 2 == 0 and screening.shape[0] <= LANES
+        and points <= LANES
+    )
+
+
 def solution(mesh):
     in_specs = (
         P(("row", "col"), None, None),
@@ -111,6 +455,11 @@
         P(("row", "col"), None),
     )
     out_specs = (P(("row", "col"), None), P())
-    return jax.shard_map(
-        on_device, mesh=mesh, in_specs=in_specs, out_specs=out_specs, check_vma=False
-    )
+
+    def run(*args):
+        body = fast_on_device if fits(args, mesh) else on_device
+        return jax.shard_map(
+            body, mesh=mesh, in_specs=in_specs, out_specs=out_specs, check_vma=False
+        )(*args)
+
+    return run

time: 301 us -> 38.5 us (0.13)
  waiting for transfers between devices: 127 us -> 0 us
  blocking collectives: 117 us -> 0 us
  Pallas kernels: 0 us -> 30.7 us
  local copies, waits for them, and re-layouts: 21.7 us -> 5.07 us
  matrix products: 16.1 us -> 0 us
  between operations: 15.6 us -> 0.67 us
    psum x1 -> x0, waiting for transfers between devices: 106 us -> none  [on_device(): density = lax.psum(partial_density, ('row', 'col'))]
    all_gather x7 -> x0, blocking collectives: 78.2 us -> none  [the longest x1 14.3 us: on_device(): lax.all_gather(valence, 'row', axis=0, tiled=True)]
    psum x1 -> x0, blocking collectives: 39.3 us -> none  [on_device(): alpha = lax.psum(gram, ('row', 'col')) / (total_count * band_count)]
    pallas_call x0 -> x1, Pallas kernels: none -> 30.7 us  [fast_on_device(): pl.pallas_call(functools.partial(kernel, (rows, cols, nk, nv, nc, nvec, t...]
    unnamed x3 -> x0, waiting for transfers between devices: 20.8 us -> none
    dot_general x28 -> x0, matrix products: 16.1 us -> none  [the longest x8 8.7 us: square_sweep(): jnp.einsum('ijg,jng->ing', coupling, col_proj, precision=highest)]
    gather x16 -> x0, local copies, waits for them, and re-layouts: 7.07 us -> none  [square_sweep(): jnp.take(lax.dynamic_slice_in_dim(screening, anchor, block_size, 1), indi...]
    dynamic_slice x8 -> x0, local copies, waits for them, and re-layouts: 5.88 us -> none  [square_sweep(): lax.dynamic_slice_in_dim(screening, anchor, block_size, 1)]
  transfers between devices with their start and end apart: 2 -> 0, of which waited for: 2 -> 0; matrix products, arithmetic and copies ran while one was open for 0% -> 0% of each run, Pallas kernels for 0% -> 0%
where the time goes in v1:
time: 38.5 us; the launch traced here: 37.9 us
  Pallas kernels  30.7 us (80%)
  local copies, waits for them, and re-layouts  5.07 us (13%)
  other arithmetic  1.46 us (4%)
  between operations  0.67 us (2%)
    pallas_call x1, Pallas kernels, fast_on_device(): pl.pallas_call(functools.partial(kernel, (rows, cols, nk, nv, nc, nvec, t...  30.7 us
    unnamed x9, local copies, waits for them, and re-layouts  3.86 us

profile of v1, /device:TPU:0, one launch (start us, length us, event | category | flops | bytes accessed | tf_op | source)
XLA Modules:
  0.0 37.9 jit_solution(14365437042015463988)
XLA Ops:
  0.6 0.8 %maximum_bitcast_fusion = bf16[2,8,8,128]{3,1,2,0:T(8,128)(2,1)S(1)} fusion(bf16[2,4,1024]{2,1,0:T(4,128)(2,1)} %param.9, bf16[2,4,1024]{2,1,0:T(4,128)(2,1)} %param.10), kind=kLoop, calls=%fused_computation.1 | loop fusion | flops 65536 | bytes 65536
  1.4 0.0 copy-start.2
  1.4 0.7 %copy-done.2 = s32[2,2]{1,0:T(2,128)S(1)} copy-done((s32[2,2]{1,0:T(2,128)S(1)}, s32[2,2]{1,0:T(2,128)}, u32[]{:S(2)}) %copy-start.2) | copy-done | bytes 40
  2.1 0.1 copy.12
  2.2 0.0 copy-start
  2.2 0.1 reshape.27
  2.3 0.1 pad.3.clone
  2.4 0.5 %copy-done = bf16[2,512]{1,0:T(2,128)(2,1)S(1)} copy-done((bf16[2,512]{1,0:T(2,128)(2,1)S(1)}, bf16[2,512]{1,0:T(2,128)(2,1)}, u32[]{:S(2)}) %copy-start) | copy-done | bytes 2072
  2.9 0.1 pad.4.clone
  3.0 0.1 maximum_maximum_fusion
  3.1 0.0 copy-start.1
  3.1 0.6 %pad_maximum_fusion.msg_ref = bf16[8,32,128]{2,1,0:T(8,128)(2,1)} fusion(bf16[8,16,128]{2,1,0:T(8,128)(2,1)S(1)} %broadcast_in_dim.22, bf16[8,16,128]{2,1,0:T(8,128)(2,1)S(1)} %bitcast.11), kind=kLoop, calls=%fused_computation | loop fusion | flops 131072 | bytes 131072 | tf_op jit(solution)/shard_map/concatenate | solution.py:295
  3.7 0.1 copy-done.1
  3.8 0.1 reshape.24
  3.8 0.1 broadcast_in_dim.23
  3.9 0.7 %reshape.25.wide_ref = f32[8,128]{1,0:T(8,128)} reshape(f32[8,4,32]{2,1,0:T(4,128)S(1)} %broadcast_in_dim.23) | data formatting | bytes 8192 | tf_op jit(solution)/shard_map/reshape | solution.py:297
  4.6 30.7 %shard_map.95 = (f32[2,512]{1,0:T(2,128)}, f32[32,32]{1,0:T(8,128)}) custom-call(bf16[8,32,128]{2,1,0:T(8,128)(2,1)} %pad_maximum_fusion.msg_ref, bf16[2,16,1024]{2,1,0:T(8,128)(2,1)} %px_ref.1, f32[8,128]{1,0:T(8,128)} %reshape.25.wide_ref, f32[1,1024]{1,0:T(1,128)} %bitcast.12, f32[34,1024]{1,0:T(8,128)} %screening_ref.1), custom_call_target="tpu_custom_call" | custom-call | tf_op jit(solution)/shard_map/pallas_call | solution.py:301
  35.3 1.3 %copy.18 = f32[2,512]{1,0:T(2,128)} copy(f32[2,512]{1,0:T(2,128)} %get-tuple-element.4) | data formatting | bytes 8192
  36.6 1.3 %copy.19 = f32[32,32]{1,0:T(8,128)} copy(f32[32,32]{1,0:T(8,128)} %get-tuple-element.5) | data formatting | bytes 8192
  (6 shorter events, 0.0 us)
Async XLA Ops:
  1.4 0.7 %copy-start.2 = (s32[2,2]{1,0:T(2,128)S(1)}, s32[2,2]{1,0:T(2,128)}, u32[]{:S(2)}) copy-start(s32[2,2]{1,0:T(2,128)} %param.15) | copy-start | bytes 52
  2.2 0.7 %copy-start = (bf16[2,512]{1,0:T(2,128)(2,1)S(1)}, bf16[2,512]{1,0:T(2,128)(2,1)}, u32[]{:S(2)}) copy-start(bf16[2,512]{1,0:T(2,128)(2,1)} %param.14) | copy-start | bytes 6148
  3.1 0.7 %copy-start.1 = (f32[2,16]{1,0:T(2,128)S(1)}, f32[2,16]{1,0:T(2,128)}, u32[]{:S(2)}) copy-start(f32[2,16]{1,0:T(2,128)} %param.13) | copy-start | bytes 388

commit v2 on v1

--- a/solution.py
+++ b/solution.py
@@ -32,8 +32,9 @@
 
 
 def kernel(
-    dims, msg_ref, px_ref, wide_ref, coulomb_ref, screening_ref,
+    dims, px_hbm, cond_hbm, val_hbm, coulomb_hbm, screening_hbm, vec_hbm, energy_hbm, place_hbm,
     out_ref, alpha_ref,
+    px_ref, cond_ref, val_ref, coulomb_ref, screening_ref, vec_ref, energy_ref, place_ref, msg_ref, wide_ref, load_sem,
     slots, px_slots, sel_v, sel_c, tile_m, block_m, perm, sel_k, screen, tiled, pairs, proj, coords, coupling,
     dens_slots, partial, out_send, out_slots, gram_slots,
     in_send, in_recv, px_send, px_recv, dens_send, dens_recv, gram_send, gram_recv, o_send, o_recv,
@@ -60,6 +61,39 @@
         return carry
 
     lax.fori_loop(1, count, greet, 0)
+
+    mine = pl.ds(pl.multiple_of(row * LANES, LANES), LANES)
+    loads = [
+        pltpu.make_async_copy(src, dst, load_sem.at[at])
+        for at, (src, dst) in enumerate((
+            (val_hbm, val_ref), (cond_hbm, cond_ref), (vec_hbm, vec_ref), (place_hbm, place_ref), (energy_hbm, energy_ref), (px_hbm, px_ref),
+            (screening_hbm.at[:, mine], screening_ref), (coulomb_hbm.at[:, mine], coulomb_ref)))
+    ]
+    for load in loads:
+        load.start()
+    for load in loads[:5]:
+        load.wait()
+    row8 = iota((8, LANES), 0)
+    lane8 = iota((8, LANES), 1)
+    spots = jnp.zeros((8, LANES), F32)
+    for axis in range(2):
+        for k in range(nk):
+            spots = jnp.where(row8 == axis * nk + k, place_ref[k, axis].astype(F32), spots)
+    energy = jnp.zeros((8, LANES), F32)
+    for k in range(nk):
+        for t in range(nb):
+            energy = jnp.where((row8 == k * nv + t // nc) & (lane8 // nvec == t % nc), energy_ref[k, t], energy)
+    vec = vec_ref[...].astype(F32)
+    packed_own = jnp.concatenate(
+        [vec[k:k + 1, j * LANES:(j + 1) * LANES] for k in range(nk) for j in range(nv)], axis=0)
+    wide_ref[0] = packed_own
+    wide_ref[1] = energy * packed_own
+    message = jnp.concatenate(
+        [ref[k].astype(F32) for k in range(nk) for ref in (val_ref, cond_ref)], axis=0).astype(BF16)
+    extra = jnp.concatenate([packed_own, spots], axis=0).astype(BF16)
+    for r in range(rows):
+        msg_ref[r, 0:16] = message[:, r * LANES:(r + 1) * LANES]
+        msg_ref[r, 16:32] = extra
 
     at = iota((batch, rows * 16), 0)
     to = iota((batch, rows * 16), 1)
@@ -79,10 +113,10 @@
     to = iota((2 * cols * kb, count * 8), 1)
     point = at % (cols * kb)
     sel_k[...] = one_hot(to == point // nk * 8 + at // (cols * kb) * nk + point % nk)
-    screen[...] = jnp.zeros_like(screen)
-    mine = pl.ds(pl.multiple_of(row * LANES, LANES), LANES)
+    for load in loads[5:]:
+        load.wait()
     high, low = split_pair(jnp.concatenate(
-        [screening_ref[:, mine], jnp.zeros((LANES - screening_ref.shape[0], LANES), F32)], axis=0))
+        [screening_ref[...], jnp.zeros((LANES - screening_ref.shape[0], LANES), F32)], axis=0))
     screen[0:LANES] = high
     screen[LANES:2 * LANES] = low
 
@@ -204,10 +238,10 @@
     density = dens_slots[0]
     for c in range(1, cols):
         density = density + dens_slots[c]
-    high, low = split_pair(density * coulomb_ref[:, mine] * (2.0 / (total * nb)))
+    high, low = split_pair(density * coulomb_ref[...] * (2.0 / (total * nb)))
     partial[...] = (dot(px, high, (1, 1)) + dot(px, low, (1, 1))).reshape(nc, rows, unit, nvec)
 
-    wide_own = wide_ref[...] * msg_ref[row, 16:32, :].astype(F32)[0:8]
+    wide_own = wide_ref[1]
     for s in range(nc):
         partial[s, row] = partial[s, row] + wide_own[:, s * nvec:(s + 1) * nvec]
 
@@ -256,7 +290,7 @@
     sums = jnp.sum(gram_slots[...], axis=0) * (1.0 / (total * nb))
     alpha = jnp.concatenate([sums[:, s * nvec:(s + 1) * nvec] for s in range(nc)], axis=0)
     alpha_ref[...] = alpha
-    own = msg_ref[row, 16:32, :].astype(F32)[0:8]
+    own = wide_ref[0]
     own_rows = jnp.concatenate([own[:, s * nvec:(s + 1) * nvec] for s in range(nc)], axis=0).astype(BF16)
     high, low = split_pair(alpha)
     taken = dot(own_rows, high, (1, 0)) + dot(own_rows, low, (1, 0))
@@ -288,25 +322,29 @@
     unit = nk * nv
     kb = rows * nk
     batch = kb * nb
-    factors = jnp.concatenate([valence, conduction], axis=1).reshape(nk * (nv + nc), rows, LANES)
-    packed = vectors.reshape(unit, LANES)
-    spots = jnp.broadcast_to(k_coords.T.astype(BF16).reshape(2 * nk, 1), (2 * nk, LANES))
-    extra = jnp.concatenate([packed, spots, jnp.zeros((16 - unit - 2 * nk, LANES), BF16)], axis=0)
-    message = jnp.concatenate(
-        [factors.transpose(1, 0, 2), jnp.broadcast_to(extra[None], (rows, 16, LANES))], axis=1)
-    wide = jnp.repeat(energies.reshape(unit, nc), nvec, axis=1)
     vmem = pl.BlockSpec(memory_space=pltpu.VMEM)
     dma = pltpu.SemaphoreType.DMA
     points = cols * kb
     return pl.pallas_call(
         functools.partial(kernel, (rows, cols, nk, nv, nc, nvec, total, total // MX)),
         out_shape=(
-            jax.ShapeDtypeStruct((nk, nb * nvec), F32),
-            jax.ShapeDtypeStruct((nvec, nvec), F32),
+            pltpu.VMEM((nk, nb * nvec), F32),
+            pltpu.VMEM((nvec, nvec), F32),
         ),
-        in_specs=[vmem] * 5,
+        in_specs=[pl.BlockSpec(memory_space=pl.ANY)] * 8,
         out_specs=(vmem, vmem),
         scratch_shapes=[
+            pltpu.VMEM(pair_exchange.shape, BF16),
+            pltpu.VMEM(conduction.shape, BF16),
+            pltpu.VMEM(valence.shape, BF16),
+            pltpu.VMEM((1, LANES), F32),
+            pltpu.VMEM((screening.shape[0], LANES), F32),
+            pltpu.VMEM(vectors.shape, BF16),
+            pltpu.SMEM(energies.shape, F32),
+            pltpu.SMEM(k_coords.shape, jnp.int32),
+            pltpu.VMEM((rows, 32, LANES), BF16),
+            pltpu.VMEM((2, unit, LANES), F32),
+            dma((8,)),
             pltpu.VMEM((cols, rows, 32, LANES), BF16),
             pltpu.VMEM((rows, nk, nb, LANES), BF16),
             pltpu.VMEM((batch, rows * 16), BF16),
@@ -333,7 +371,7 @@
             dma((rows,)), dma((rows,)),
         ],
         compiler_params=pltpu.CompilerParams(collective_id=0, has_side_effects=True),
-    )(message, pair_exchange, wide, coulomb.reshape(1, planes), screening)
+    )(pair_exchange, conduction, valence, coulomb.reshape(1, planes), screening, vectors, energies, k_coords)
 
 
 highest = lax.Precision.HIGHEST

time: 38.5 us -> 31.6 us (0.82)
  local copies, waits for them, and re-layouts: 5.07 us -> 1.2 us
  other arithmetic: 1.46 us -> 0 us
  Pallas kernels: 30.7 us -> 29.5 us
    unnamed x9 -> x2, local copies, waits for them, and re-layouts: 3.86 us -> 1.2 us
    pallas_call x1, Pallas kernels: 30.7 us -> 29.5 us  [fast_on_device(): pl.pallas_call(functools.partial(kernel, (rows, cols, nk, nv, nc, nvec, t...]
    reshape x4 -> x0, local copies, waits for them, and re-layouts: 0.77 us -> none  [the longest x2 0.76 us: fast_on_device(): wide = jnp.repeat(energies.reshape(unit, nc), nvec, axis=1)]
    unnamed x1 -> x0, other arithmetic: 0.76 us -> none
    concatenate x2 -> x0, other arithmetic: 0.7 us -> none  [the longest x1 0.62 us: fast_on_device(): jnp.concatenate([factors.transpose(1, 0, 2), jnp.broadcast_to(extra[None]...]
where the time goes in v2:
time: 31.6 us; the launch traced here: 31.3 us
  Pallas kernels  29.5 us (93%)
  local copies, waits for them, and re-layouts  1.2 us (4%)
  between operations  0.64 us (2%)
    pallas_call x1, Pallas kernels, fast_on_device(): pl.pallas_call(functools.partial(kernel, (rows, cols, nk, nv, nc, nvec, t...  29.5 us
    unnamed x2, local copies, waits for them, and re-layouts  1.2 us

profile of v2, /device:TPU:0, one launch (start us, length us, event | category | flops | bytes accessed | tf_op | source)
XLA Modules:
  0.0 31.3 jit_solution(2613556106648246020)
XLA Ops:
  0.6 29.5 %shard_map.95 = (f32[2,512]{1,0:T(2,128)S(1)}, f32[32,32]{1,0:T(8,128)S(1)}) custom-call(bf16[2,16,1024]{2,1,0:T(8,128)(2,1)} %px_hbm.1, bf16[2,4,1024]{2,1,0:T(4,128)(2,1)} %cond_hbm.1, bf16[2,4,1024]{2,1,0:T(4,128)(2,1)} %val_hbm.1, f32[1,1024]{1,0:T(1,128)} %bitcast.1, f32[34,1024]{1,0:T(8,128)} %screening_hbm.1, bf16[2,512]{1,0:T(2,128)(2,1)} %vec_hbm.1, ...), custom_call_target="tpu_custom_call" | custom-call | tf_op jit(solution)/shard_map/pallas_call | solution.py:328
  30.1 0.6 %copy.12 = f32[2,512]{1,0:T(2,128)} copy(f32[2,512]{1,0:T(2,128)S(1)} %get-tuple-element.2) | data formatting | bytes 8192
  30.7 0.6 %copy.13 = f32[32,32]{1,0:T(8,128)} copy(f32[32,32]{1,0:T(8,128)S(1)} %get-tuple-element.3) | data formatting | bytes 8192

commit v3 on v2

--- a/solution.py
+++ b/solution.py
@@ -55,12 +55,10 @@
 
     barrier = pltpu.get_barrier_semaphore()
 
-    def greet(step, carry):
-        pr, pc = other(step)
-        pl.semaphore_signal(barrier, inc=1, device_id=(pr, pc), device_id_type=MESH)
-        return carry
-
-    lax.fori_loop(1, count, greet, 0)
+    for step in range(1, rows):
+        pl.semaphore_signal(barrier, inc=1, device_id=(lax.rem(row + step, rows), col), device_id_type=MESH)
+    for step in range(1, cols):
+        pl.semaphore_signal(barrier, inc=1, device_id=(row, lax.rem(col + step, cols)), device_id_type=MESH)
 
     mine = pl.ds(pl.multiple_of(row * LANES, LANES), LANES)
     loads = [
@@ -115,19 +113,27 @@
     sel_k[...] = one_hot(to == point // nk * 8 + at // (cols * kb) * nk + point % nk)
     for load in loads[5:]:
         load.wait()
+    slots[col, row] = msg_ref[row]
     high, low = split_pair(jnp.concatenate(
         [screening_ref[...], jnp.zeros((LANES - screening_ref.shape[0], LANES), F32)], axis=0))
     screen[0:LANES] = high
     screen[LANES:2 * LANES] = low
 
-    pl.semaphore_wait(barrier, count - 1)
+    pl.semaphore_wait(barrier, rows + cols - 2)
 
     def in_copy(step):
-        pr, pc = other(step)
+        pr = lax.rem(row + step, rows)
         return pltpu.make_async_remote_copy(
             src_ref=msg_ref.at[pr], dst_ref=slots.at[col, row],
-            send_sem=in_send.at[pc, pr], recv_sem=in_recv.at[col, row],
-            device_id=(pr, pc), device_id_type=MESH)
+            send_sem=in_send.at[col, pr], recv_sem=in_recv.at[col, row],
+            device_id=(pr, col), device_id_type=MESH)
+
+    def relay_copy(r, step):
+        pc = lax.rem(col + step, cols)
+        return pltpu.make_async_remote_copy(
+            src_ref=slots.at[col, r], dst_ref=slots.at[col, r],
+            send_sem=in_send.at[pc, r], recv_sem=in_recv.at[col, r],
+            device_id=(row, pc), device_id_type=MESH)
 
     def px_copy(step):
         pr = lax.rem(row + step, rows)
@@ -166,18 +172,22 @@
     def landed(ref, sem):
         pltpu.make_async_copy(ref, ref, sem).wait()
 
+    start_all(in_copy, rows)
     start_all(px_copy, rows)
-    start_all(in_copy, count)
-    slots[col, row] = msg_ref[row]
     px_slots[row] = px_ref[:, :, mine]
 
+    def relay(d, carry):
+        r = lax.rem(row + d, rows)
+        landed(slots.at[col, r], in_recv.at[col, r])
+        for step in range(1, cols):
+            relay_copy(r, step).start()
+        return carry
+
+    for step in range(1, cols):
+        relay_copy(row, step).start()
+    lax.fori_loop(1, rows, relay, 0)
+
     def take_batch(which):
-        def wait_one(r, carry):
-            @pl.when((r != row) | (which != col))
-            def _():
-                landed(slots.at[which, r], in_recv.at[which, r])
-            return carry
-        lax.fori_loop(0, rows, wait_one, 0)
         got = slots[which]
         factors = got[:, 0:16, :].reshape(rows * 16, LANES)
         rest = got[:, 16:32, :].astype(F32)
@@ -206,7 +216,14 @@
     start_all(dens_copy, cols)
 
     def rest_batches(step, carry):
-        take_batch(lax.rem(col + step, cols))
+        c = lax.rem(col + step, cols)
+
+        def wait_one(r, inner):
+            landed(slots.at[c, r], in_recv.at[c, r])
+            return inner
+
+        lax.fori_loop(0, rows, wait_one, 0)
+        take_batch(c)
         return carry
 
     lax.fori_loop(1, cols, rest_batches, 0)
@@ -305,7 +322,14 @@
             return carry
         lax.fori_loop(1, end, body, 0)
 
-    drain(in_copy, count)
+    drain(in_copy, rows)
+
+    def drain_relay(r, carry):
+        for step in range(1, cols):
+            relay_copy(r, step).wait_send()
+        return carry
+
+    lax.fori_loop(0, rows, drain_relay, 0)
     drain(px_copy, rows)
     drain(dens_copy, cols)
     drain(o_copy, rows)

time: 31.6 us -> 27.9 us (0.88)
  Pallas kernels: 29.5 us -> 25.8 us
    pallas_call x1, Pallas kernels: 29.5 us -> 25.8 us  [fast_on_device(): pl.pallas_call(functools.partial(kernel, (rows, cols, nk, nv, nc, nvec, t...]
where the time goes in v3:
time: 27.9 us; the launch traced here: 27.6 us
  Pallas kernels  25.8 us (92%)
  local copies, waits for them, and re-layouts  1.2 us (4%)
  between operations  0.64 us (2%)
    pallas_call x1, Pallas kernels, fast_on_device(): pl.pallas_call(functools.partial(kernel, (rows, cols, nk, nv, nc, nvec, t...  25.8 us
    unnamed x2, local copies, waits for them, and re-layouts  1.2 us

profile of v3, /device:TPU:0, one launch (start us, length us, event | category | flops | bytes accessed | tf_op | source)
XLA Modules:
  0.0 27.6 jit_solution(1701877850019500293)
XLA Ops:
  0.6 25.8 %shard_map.95 = (f32[2,512]{1,0:T(2,128)S(1)}, f32[32,32]{1,0:T(8,128)S(1)}) custom-call(bf16[2,16,1024]{2,1,0:T(8,128)(2,1)} %px_hbm.1, bf16[2,4,1024]{2,1,0:T(4,128)(2,1)} %cond_hbm.1, bf16[2,4,1024]{2,1,0:T(4,128)(2,1)} %val_hbm.1, f32[1,1024]{1,0:T(1,128)} %bitcast.1, f32[34,1024]{1,0:T(8,128)} %screening_hbm.1, bf16[2,512]{1,0:T(2,128)(2,1)} %vec_hbm.1, ...), custom_call_target="tpu_custom_call" | custom-call | tf_op jit(solution)/shard_map/pallas_call | solution.py:352
  26.4 0.6 %copy.12 = f32[2,512]{1,0:T(2,128)} copy(f32[2,512]{1,0:T(2,128)S(1)} %get-tuple-element.2) | data formatting | bytes 8192
  27.0 0.6 %copy.13 = f32[32,32]{1,0:T(8,128)} copy(f32[32,32]{1,0:T(8,128)S(1)} %get-tuple-element.3) | data formatting | bytes 8192

commit v4 on v3

--- a/solution.py
+++ b/solution.py
@@ -124,14 +124,18 @@
     def in_copy(step):
         pr = lax.rem(row + step, rows)
         return pltpu.make_async_remote_copy(
-            src_ref=msg_ref.at[pr], dst_ref=slots.at[col, row],
+            src_ref=msg_ref.at[pr, 0:28], dst_ref=slots.at[col, row, 0:28],
             send_sem=in_send.at[col, pr], recv_sem=in_recv.at[col, row],
             device_id=(pr, col), device_id_type=MESH)
 
+    def across(step):
+        far = lax.rem(col // 2 + step // 2, cols // 2)
+        return far * 2 + lax.rem(lax.rem(col, 2) + lax.rem(step, 2), 2)
+
     def relay_copy(r, step):
-        pc = lax.rem(col + step, cols)
+        pc = across(step)
         return pltpu.make_async_remote_copy(
-            src_ref=slots.at[col, r], dst_ref=slots.at[col, r],
+            src_ref=slots.at[col, r, 0:28], dst_ref=slots.at[col, r, 0:28],
             send_sem=in_send.at[pc, r], recv_sem=in_recv.at[col, r],
             device_id=(row, pc), device_id_type=MESH)
 
@@ -178,7 +182,7 @@
 
     def relay(d, carry):
         r = lax.rem(row + d, rows)
-        landed(slots.at[col, r], in_recv.at[col, r])
+        landed(slots.at[col, r, 0:28], in_recv.at[col, r])
         for step in range(1, cols):
             relay_copy(r, step).start()
         return carry
@@ -192,7 +196,8 @@
         factors = got[:, 0:16, :].reshape(rows * 16, LANES)
         rest = got[:, 16:32, :].astype(F32)
         packed = rest[:, 0:8, :].reshape(per, LANES).astype(BF16)
-        coords[which] = rest[:, 8:16, :].reshape(rows * 8, LANES).astype(BF16)
+        spots_in = rest[:, 8:16, :].reshape(rows * 8, LANES)
+        coords[which] = jnp.where(iota(spots_in.shape, 0) % 8 < 4, spots_in, 0.0).astype(BF16)
         wide = dot(packed, tile_m[...], (1, 0)).astype(BF16)
         stacked = jnp.concatenate([wide[:, s * LANES:(s + 1) * LANES] for s in range(nc)], axis=0)
         tiled[which] = stacked
@@ -216,10 +221,10 @@
     start_all(dens_copy, cols)
 
     def rest_batches(step, carry):
-        c = lax.rem(col + step, cols)
+        c = across(step)
 
         def wait_one(r, inner):
-            landed(slots.at[c, r], in_recv.at[c, r])
+            landed(slots.at[c, r, 0:28], in_recv.at[c, r])
             return inner
 
         lax.fori_loop(0, rows, wait_one, 0)
@@ -500,7 +505,7 @@
     nvec = vectors.shape[1] // nb
     return (
         planes == rows * LANES and nc * nvec == LANES and nk * nv == 8 and nk * (nv + nc) == 16
-        and nk == 2 and nvec // nc == 8 and rows % 2 == 0 and screening.shape[0] <= LANES
+        and nk == 2 and nvec // nc == 8 and rows % 2 == 0 and cols % 2 == 0 and screening.shape[0] <= LANES
         and points <= LANES
     )
 

time: 27.9 us -> 27.4 us (0.982)
  Pallas kernels: 25.8 us -> 25.3 us
    pallas_call x1, Pallas kernels: 25.8 us -> 25.3 us  [fast_on_device(): pl.pallas_call(functools.partial(kernel, (rows, cols, nk, nv, nc, nvec, t...]
where the time goes in v4:
time: 27.4 us; the launch traced here: 27.2 us
  Pallas kernels  25.3 us (92%)
  local copies, waits for them, and re-layouts  1.2 us (4%)
  between operations  0.64 us (2%)
    pallas_call x1, Pallas kernels, fast_on_device(): pl.pallas_call(functools.partial(kernel, (rows, cols, nk, nv, nc, nvec, t...  25.3 us
    unnamed x2, local copies, waits for them, and re-layouts  1.2 us

profile of v4, /device:TPU:0, one launch (start us, length us, event | category | flops | bytes accessed | tf_op | source)
XLA Modules:
  0.0 27.2 jit_solution(8345826170451266519)
XLA Ops:
  0.6 25.3 %shard_map.95 = (f32[2,512]{1,0:T(2,128)S(1)}, f32[32,32]{1,0:T(8,128)S(1)}) custom-call(bf16[2,16,1024]{2,1,0:T(8,128)(2,1)} %px_hbm.1, bf16[2,4,1024]{2,1,0:T(4,128)(2,1)} %cond_hbm.1, bf16[2,4,1024]{2,1,0:T(4,128)(2,1)} %val_hbm.1, f32[1,1024]{1,0:T(1,128)} %bitcast.1, f32[34,1024]{1,0:T(8,128)} %screening_hbm.1, bf16[2,512]{1,0:T(2,128)(2,1)} %vec_hbm.1, ...), custom_call_target="tpu_custom_call" | custom-call | tf_op jit(solution)/shard_map/pallas_call | solution.py:357
  26.0 0.6 %copy.12 = f32[2,512]{1,0:T(2,128)} copy(f32[2,512]{1,0:T(2,128)S(1)} %get-tuple-element.2) | data formatting | bytes 8192
  26.6 0.6 %copy.13 = f32[32,32]{1,0:T(8,128)} copy(f32[32,32]{1,0:T(8,128)S(1)} %get-tuple-element.3) | data formatting | bytes 8192
